TPU v7x, 32 devices: a whole 2x2x4 slice. The times are simulated.
32 devices in a mesh: groups: 2 (over y), seq: 4 (over z), head: 2 (over x), rep: 2 (over core).
Axes of the slice: x: 2, y: 2, z: 4, core: 2. Of those that a mesh axis runs over, the one named last changes fastest.
Arguments:
- kv_cache: bfloat16 [2, 256, 8, 128, 256], P(None, ('groups', 'seq'), 'head', 'rep'), parts along dimension 1, may hold values from -6 to 6
- keep_list: int32 [4, 64], P('groups'), parts along dimension 0, may hold values from -1 to 127, as said below
- page_slot: int32 [4, 64], P('groups'), parts along dimension 0, may hold values from -1 to 63, as said below
Outputs:
- paged_cache: bfloat16 [2, 128, 8, 128, 256], P(None, ('groups', 'seq'), 'head', 'rep'), parts along dimension 1
- page_bounds: bfloat16 [2, 128, 8, 2, 128], P(None, ('groups', 'seq'), 'head'), parts along dimension 1
There are 2 independent parts, one for each index of `groups`. A program takes and returns all parts, laid end to end along the dimension named above; each array names one. Nothing has to cross between parts.
Inputs may be any that keep to these rules, and one draw needn't show every extreme that they name: `keep_list`: row l holds count_l distinct block indices in rising order, then -1 in the remaining entries. Of one row, at most 16 listed blocks lie on one seq shard (blocks s * 32 to s * 32 + 31); row 0 reaches this on every shard. `page_slot`: entry (l, j) is the page of block keep_list[l, j]: distinct pages for the count_l listed blocks of a row, -1 after them. Of one row, at most 5 blocks of one seq shard go to pages of one owner (pages o * 16 to o * 16 + 15), and this is reached in every draw.
All inputs are finite; a program needn't handle non-finite values.
Results may differ from a plain program's by a relative error of at most 0.001.
Values may be sent and summed in bfloat16 or wider, within the bound.
A program may use at most 64 MiB of HBM per device.

v0:
```python
import jax
import jax.numpy as jnp
from jax import lax
from jax.sharding import PartitionSpec as P


def combined_all(part, axis, combine):
    gathered = jax.tree.map(lambda a: lax.all_gather(a, axis), part)

    def take(source):
        return jax.tree.map(lambda a: lax.dynamic_index_in_dim(a, source, 0, False), gathered)

    return lax.fori_loop(
        1, lax.axis_size(axis), lambda source, state: combine(state, take(source)), take(0)
    )


def pack_slots(block_rows, sent_here, destination, local_block, slot_width):
    blk_dev = block_rows.shape[1]
    slot_hot = (
        destination[:, :, None] == jnp.arange(slot_width, dtype=jnp.int32)[None, None, :]
    ) & sent_here[:, :, None]
    block_hot = local_block[:, :, None] == jnp.arange(blk_dev, dtype=jnp.int32)[None, None, :]
    select = jnp.einsum(
        "ljw,ljb->lwb", slot_hot.astype(jnp.float32), block_hot.astype(jnp.float32)
    ).astype(jnp.bfloat16)
    return jnp.einsum(
        "lwb,lbr->lwr", select, block_rows, preferred_element_type=jnp.float32
    ).astype(jnp.bfloat16)


def place_index(takers, in_page, incoming, page_dev):
    page_hot = (
        in_page[:, :, None] == jnp.arange(page_dev, dtype=jnp.int32)[None, None, :]
    ) & takers[:, :, None]
    return jnp.sum(jnp.where(page_hot, incoming[:, :, None] + 1, 0), axis=1) - 1


def place_pages(target, shard_part):
    width = shard_part.shape[1]
    one_hot = (target[:, :, None] == jnp.arange(width, dtype=jnp.int32)[None, None, :]).astype(
        jnp.bfloat16
    )
    return jnp.einsum("lpn,lnr->lpr", one_hot, shard_part, preferred_element_type=jnp.float32)


def extend(first, second):
    return (jnp.maximum(first[0], second[0]), jnp.minimum(first[1], second[1]))


def on_device(kv_cache, keep_list, page_slot):
    layer_count, page_count = keep_list.shape
    blk_dev = kv_cache.shape[1]
    seq_count = lax.axis_size("seq")
    page_dev = page_count // seq_count
    capacity = (page_dev - 2) // seq_count + 2
    seq_index = lax.axis_index("seq")
    block_rows = kv_cache.reshape(layer_count, blk_dev, -1)
    position = jnp.arange(page_count, dtype=jnp.int32)
    counts = jnp.array(
        [page_count - layer * page_count // (2 * layer_count) for layer in range(layer_count)],
        jnp.int32,
    )
    listed = position[None, :] < counts[:, None]
    source = keep_list // blk_dev
    local_block = keep_list % blk_dev
    owner_index = page_slot // page_dev
    in_page = page_slot % page_dev
    earlier = (position[None, None, :] < position[None, :, None]) & listed[:, None, :]
    same_source = source[:, :, None] == source[:, None, :]
    sent_here = listed & (source == seq_index)
    takers = listed & (owner_index == seq_index)
    same_owner = owner_index[:, :, None] == owner_index[:, None, :]
    slot_rank = jnp.sum(earlier & same_source & same_owner, axis=2)
    packed = pack_slots(
        block_rows, sent_here, owner_index * capacity + slot_rank, local_block, seq_count * capacity
    )
    received = lax.all_to_all(packed, "seq", split_axis=1, concat_axis=1, tiled=True)
    target = place_index(takers, in_page, source * capacity + slot_rank, page_dev)
    gathered = place_pages(target, received)
    paged_cache = gathered.astype(jnp.bfloat16).reshape(
        (layer_count, page_dev) + kv_cache.shape[2:]
    )
    head_width = kv_cache.shape[-1] // 2
    key_part = paged_cache[..., :head_width]
    key_high = jnp.max(key_part, axis=3)
    key_low = jnp.min(key_part, axis=3)
    upper_bound, lower_bound = combined_all((key_high, key_low), "rep", extend)
    page_bounds = jnp.stack([upper_bound, lower_bound], axis=3)
    return (paged_cache, page_bounds)


def solution(mesh):
    in_specs = (
        P(None, ("groups", "seq"), "head", "rep", None),
        P("groups", None),
        P("groups", None),
    )
    out_specs = (
        P(None, ("groups", "seq"), "head", "rep", None),
        P(None, ("groups", "seq"), "head", None, None),
    )
    return jax.shard_map(
        on_device, mesh=mesh, in_specs=in_specs, out_specs=out_specs, check_vma=False
    )
```

profile of v0, /device:TPU:0, one launch (start us, length us, event | category | flops | bytes accessed | tf_op | source)
XLA Modules:
  0.0 169.5 jit_solution(9701776969983335946)
XLA Ops:
  0.7 0.8 compare_and_fusion
  1.4 0.2 convert_reduce_fusion
  1.6 0.7 add_add_fusion
  2.3 10.6 %reshape.91 = bf16[2,32,65536]{2,1,0:T(8,128)(2,1)} reshape(bf16[2,32,4,64,256]{4,3,2,1,0:T(8,128)(2,1)} %param.4) | data formatting | bytes 16777216 | tf_op jit(solution)/shard_map/reshape | solution.py:58
  12.9 8.5 %convolution_convert_fusion = bf16[2,20,65536]{2,1,0:T(8,128)(2,1)} fusion(bf16[2,32,65536]{2,1,0:T(8,128)(2,1)} %reshape.91, s32[2,64]{1,0:T(2,128)S(1)} %get-tuple-element.38, s32[2,64]{1,0:T(2,128)S(1)} %get-tuple-element.33, pred[2,64]{1,0:T(4,128)(4,1)S(1)} %get-tuple-element.30), kind=kOutput, calls=%fused_computation | convolution fusion | flops 170567936 | bytes 13632640 | tf_op jit(solution)/shard_map/lwb,lbr->lwr/dot_general | solution.py:27
  21.4 9.0 %copy.12 = bf16[2,20,65536]{2,0,1:T(2,128)(2,1)} copy(bf16[2,20,65536]{2,1,0:T(8,128)(2,1)} %convolution_convert_fusion) | data formatting | bytes 10485760 | tf_op jit(solution)/shard_map/convert_element_type | solution.py:29
  30.4 0.0 copy-start.1
  30.4 6.5 %all-to-all-start = ((bf16[2,20,65536]{2,0,1:T(2,128)(2,1)}), bf16[2,20,65536]{2,0,1:T(2,128)(2,1)}, u32[]{:S(2)}, u32[]{:S(2)}) async-start(bf16[2,20,65536]{2,0,1:T(2,128)(2,1)} %copy.12), calls=%async_computation | async-start | bytes 10485760 | tf_op jit(solution)/shard_map/all_to_all | solution.py:78
  36.8 0.0 copy-done.1
  36.9 0.1 select_reduce_fusion
  37.0 116.2 %all-to-all-done = bf16[2,20,65536]{2,0,1:T(2,128)(2,1)} async-done(((bf16[2,20,65536]{2,0,1:T(2,128)(2,1)}), bf16[2,20,65536]{2,0,1:T(2,128)(2,1)}, u32[]{:S(2)}, u32[]{:S(2)}) %all-to-all-start) | async-done | bytes 5242912 | tf_op jit(solution)/shard_map/all_to_all | solution.py:78
  153.2 9.3 %convolution_convert_fusion.1 = bf16[2,16,65536]{2,1,0:T(8,128)(2,1)S(1)} fusion(bf16[2,20,65536]{2,0,1:T(2,128)(2,1)} %all-to-all-done, s32[2,16]{1,0:T(2,128)S(1)} %broadcast_add_fusion), kind=kOutput, calls=%fused_computation.1 | convolution fusion | flops 85983872 | bytes 9437312 | tf_op jit(solution)/shard_map/lpn,lnr->lpr/dot_general | solution.py:44
  162.5 1.0 copy.17
  163.5 0.0 copy-start
  163.5 1.5 slice_reduce_fusion.1
  165.0 1.9 %all-gather = bf16[4,16,4,128]{3,1,2,0:T(8,128)(2,1)S(1)} all-gather(bf16[2,16,4,128]{3,1,2,0:T(8,128)(2,1)S(1)} %copy.14), channel_id=2, replica_groups=mesh['groups'=2,'seq'=4,'head'=2,'rep'=2] {'rep'}, dimensions={0}, use_global_device_ids=true | all-gather | bytes 98304 | tf_op jit(solution)/shard_map/all_gather | solution.py:8
  166.9 1.9 %all-gather.1 = bf16[4,16,4,128]{3,1,2,0:T(8,128)(2,1)S(1)} all-gather(bf16[2,16,4,128]{3,1,2,0:T(8,128)(2,1)S(1)} %copy.15), channel_id=3, replica_groups=mesh['groups'=2,'seq'=4,'head'=2,'rep'=2] {'rep'}, dimensions={0}, use_global_device_ids=true | all-gather | bytes 98304 | tf_op jit(solution)/shard_map/all_gather | solution.py:8
  168.8 0.7 copy.16
  169.5 0.0 copy-done
  (8 shorter events, 0.1 us)
Async XLA Ops:
  30.4 6.5 %copy-start.1 = (s32[2,64]{1,0:T(2,128)S(1)}, s32[2,64]{1,0:T(2,128)}, u32[]{:S(2)}) copy-start(s32[2,64]{1,0:T(2,128)} %param.6) | copy-start | bytes 1540
  30.4 122.8 %all-to-all-start = ((bf16[2,20,65536]{2,0,1:T(2,128)(2,1)}), bf16[2,20,65536]{2,0,1:T(2,128)(2,1)}, u32[]{:S(2)}, u32[]{:S(2)}) async-start(bf16[2,20,65536]{2,0,1:T(2,128)(2,1)} %copy.12), calls=%async_computation | async-start | bytes 10485760 | tf_op jit(solution)/shard_map/all_to_all | solution.py:78
  163.5 6.0 %copy-start = (bf16[4,8,256,256]{3,2,1,0:T(8,128)(2,1)}, bf16[4,8,256,256]{3,2,1,0:T(8,128)(2,1)S(1)}, u32[]{:S(2)}) copy-start(bf16[4,8,256,256]{3,2,1,0:T(8,128)(2,1)S(1)} %copy.17) | copy-start | bytes 12582916
where the time goes:
time: 170 us; the launch traced here: 169 us
  waiting for transfers between devices  116 us (68%)
  local copies, waits for them, and re-layouts  21.2 us (12%)
  matrix products  17.8 us (10%)
  starting transfers between devices  6.48 us (4%)
  blocking collectives  3.71 us (2%)
  other arithmetic  3.36 us (2%)
    all_to_all x1, waiting for transfers between devices, on_device(): lax.all_to_all(packed, 'seq', split_axis=1, concat_axis=1, tiled=True)  116 us
    reshape x1, local copies, waits for them, and re-layouts, on_device(): block_rows = kv_cache.reshape(layer_count, blk_dev, -1)  10.6 us
    dot_general x1, matrix products, place_pages(): jnp.einsum('lpn,lnr->lpr', one_hot, shard_part, preferred_element_type=jn...  9.26 us
    convert_element_type x1, local copies, waits for them, and re-layouts, pack_slots(): return jnp.einsum('lwb,lbr->lwr', select, block_rows, preferred_element_t...  8.97 us
    dot_general x1, matrix products, pack_slots(): jnp.einsum('lwb,lbr->lwr', select, block_rows, preferred_element_type=jnp...  8.5 us
    all_to_all x1, starting transfers between devices, on_device(): lax.all_to_all(packed, 'seq', split_axis=1, concat_axis=1, tiled=True)  6.48 us
    all_gather x2, blocking collectives, combined_all(): gathered = jax.tree.map(lambda a: lax.all_gather(a, axis), part)  3.71 us
  transfers between devices with their start and end apart: 1, of which 1 were waited for; matrix products, arithmetic and copies ran while one was open for 0% of the time, Pallas kernels for 0%

commit v1 on v0

--- a/solution.py
+++ b/solution.py
@@ -1,7 +1,18 @@
+import functools
+
 import jax
 import jax.numpy as jnp
 from jax import lax
+from jax.experimental import pallas as pl
+from jax.experimental.pallas import tpu as pltpu
 from jax.sharding import PartitionSpec as P
+
+MESH = pl.DeviceIdType.MESH
+ANY = pl.BlockSpec(memory_space=pl.ANY)
+SMEM = pl.BlockSpec(memory_space=pltpu.SMEM)
+VMEM = pl.BlockSpec(memory_space=pltpu.VMEM)
+
+SHARED = (2, 3, 4, 5)
 
 
 def combined_all(part, axis, combine):
@@ -48,7 +59,7 @@
     return (jnp.maximum(first[0], second[0]), jnp.minimum(first[1], second[1]))
 
 
-def on_device(kv_cache, keep_list, page_slot):
+def any_line(kv_cache, keep_list, page_slot):
     layer_count, page_count = keep_list.shape
     blk_dev = kv_cache.shape[1]
     seq_count = lax.axis_size("seq")
@@ -90,6 +101,398 @@
     return (paged_cache, page_bounds)
 
 
+def pack_kernel(table, blocks, packed, held, read_sem, write_sem):
+    count = packed.shape[0]
+
+    def read(k):
+        return pltpu.make_async_copy(blocks.at[table[k]], held.at[k], read_sem.at[k])
+
+    def write(k):
+        return pltpu.make_async_copy(held.at[k], packed.at[k], write_sem.at[k])
+
+    @pl.loop(0, count)
+    def _(k):
+        read(k).start()
+
+    @pl.loop(0, count)
+    def _(k):
+        read(k).wait()
+        write(k).start()
+
+    @pl.loop(0, count)
+    def _(k):
+        write(k).wait()
+
+
+def place_kernel(table, slots, bounds, pages, page_bounds, held, read_sem, write_sem):
+    count = pages.shape[0]
+
+    def read(k):
+        return pltpu.make_async_copy(slots.at[table[k]], held.at[k], read_sem.at[k])
+
+    def write(k):
+        return pltpu.make_async_copy(held.at[k], pages.at[k], write_sem.at[k])
+
+    @pl.loop(0, count)
+    def _(k):
+        read(k).start()
+
+    @pl.loop(0, count)
+    def _(k):
+        page_bounds[k] = bounds[table[k]]
+
+    @pl.loop(0, count)
+    def _(k):
+        read(k).wait()
+        write(k).start()
+
+    @pl.loop(0, count)
+    def _(k):
+        write(k).wait()
+
+
+def exchange_kernel(
+    cap, shared, packed, slots, bounds,
+    held, mine, theirs, send_sem, recv_sem, relay_sem, local_sem, write_sem, rep_send, rep_recv,
+):
+    me = lax.axis_index("seq")
+    half, lane = me // 2, me % 2
+    partner = me + 1 - 2 * lane
+    near, far = 2 - half, 3 - 3 * half
+    inner = half + lane == 1
+    other = 1 - lax.axis_index("rep")
+    alone = cap - shared
+    heads, width = held.shape[1], mine.shape[2]
+
+    barrier = pltpu.get_barrier_semaphore()
+    for step in range(1, 4):
+        pl.semaphore_signal(
+            barrier, inc=1, device_id={"seq": (me + step) % 4}, device_id_type=MESH
+        )
+    pl.semaphore_signal(barrier, inc=1, device_id={"rep": other}, device_id_type=MESH)
+    pl.semaphore_wait(barrier, 4)
+
+    def remote(source, place, target, sem):
+        return pltpu.make_async_remote_copy(
+            src_ref=source,
+            dst_ref=held.at[place],
+            send_sem=sem,
+            recv_sem=recv_sem.at[place],
+            device_id={"seq": target},
+            device_id_type=MESH,
+        )
+
+    def to_near(q):
+        return remote(packed.at[q], lane * cap + q, near, send_sem.at[q])
+
+    def to_far(q):
+        return remote(packed.at[q + alone], lane * cap + q, far, send_sem.at[q + alone])
+
+    def to_partner(q):
+        return remote(packed.at[2 * cap + q], 2 * cap + q, partner, send_sem.at[2 * cap + q])
+
+    def relay(place, sem):
+        return remote(held.at[place], place, partner, relay_sem.at[sem])
+
+    def landed(place):
+        pltpu.make_async_copy(held.at[place], held.at[place], recv_sem.at[place]).wait()
+
+    def own(q):
+        return pltpu.make_async_copy(
+            packed.at[3 * cap + q], held.at[3 * cap + q], local_sem.at[q]
+        )
+
+    def write(place):
+        return pltpu.make_async_copy(held.at[place], slots.at[place], write_sem.at[place])
+
+    def finish(place):
+        keys = held[place, :, :, :width].astype(jnp.float32)
+        mine[place, :heads] = jnp.max(keys, axis=1)
+        mine[place, heads:] = jnp.min(keys, axis=1)
+        write(place).start()
+
+    def swap(start, count, k):
+        return pltpu.make_async_remote_copy(
+            src_ref=mine.at[pl.ds(start, count)],
+            dst_ref=theirs.at[pl.ds(start, count)],
+            send_sem=rep_send.at[k],
+            recv_sem=rep_recv.at[k],
+            device_id={"rep": other},
+            device_id_type=MESH,
+        )
+
+    def join(start, count):
+        @pl.loop(0, count)
+        def _(q):
+            a, b = mine[start + q], theirs[start + q]
+            bounds[start + q, :heads] = jnp.maximum(a[:heads], b[:heads])
+            bounds[start + q, heads:] = jnp.minimum(a[heads:], b[heads:])
+
+    @pl.when(jnp.logical_not(inner))
+    def _():
+        @pl.loop(0, cap)
+        def _(q):
+            to_partner(q).start()
+
+    @pl.loop(0, shared)
+    def _(q):
+        to_near(q).start()
+
+    @pl.loop(shared, cap)
+    def _(q):
+        to_far(q).start()
+        to_near(q).start()
+
+    @pl.when(inner)
+    def _():
+        @pl.loop(0, cap)
+        def _(q):
+            to_partner(q).start()
+
+    @pl.loop(0, cap)
+    def _(q):
+        own(q).start()
+
+    empty = 4 * cap
+    held[empty] = jnp.zeros(held.shape[1:], held.dtype)
+    bounds[empty] = jnp.zeros(bounds.shape[1:], bounds.dtype)
+
+    @pl.loop(0, cap)
+    def _(q):
+        own(q).wait()
+        finish(3 * cap + q)
+
+    write(empty).start()
+    first, second = half * cap, (1 - half) * cap
+
+    if shared:
+        @pl.when(inner)
+        def _():
+            @pl.loop(0, shared)
+            def _(q):
+                landed(first + q)
+                relay(first + q, q).start()
+
+            @pl.loop(0, shared)
+            def _(q):
+                landed(second + q)
+                relay(second + q, shared + q).start()
+
+    @pl.loop(0, cap)
+    def _(q):
+        landed(2 * cap + q)
+        finish(2 * cap + q)
+
+    swap(2 * cap, 2 * cap, 0).start()
+
+    def collect(start):
+        if shared:
+            @pl.when(jnp.logical_not(inner))
+            def _():
+                @pl.loop(0, shared)
+                def _(q):
+                    landed(start + q)
+
+            @pl.loop(0, shared)
+            def _(q):
+                finish(start + q)
+
+        @pl.loop(shared, cap)
+        def _(q):
+            landed(start + q)
+            finish(start + q)
+
+    collect(first)
+    swap(2 * cap, 2 * cap, 0).wait()
+    join(2 * cap, 2 * cap)
+    swap(first, cap, 1).start()
+    collect(second)
+
+    @pl.loop(2 * cap, 4 * cap + 1)
+    def _(k):
+        write(k).wait()
+
+    @pl.loop(0, cap)
+    def _(q):
+        write(first + q).wait()
+
+    swap(second, cap, 2).start()
+    swap(first, cap, 1).wait()
+    join(first, cap)
+
+    @pl.loop(0, 2 * cap - shared)
+    def _(q):
+        to_near(q).wait_send()
+
+    @pl.loop(0, cap)
+    def _(q):
+        to_partner(q).wait_send()
+        write(second + q).wait()
+
+    if shared:
+        @pl.when(inner)
+        def _():
+            @pl.loop(0, shared)
+            def _(q):
+                relay(first + q, q).wait_send()
+                relay(second + q, shared + q).wait_send()
+
+    swap(second, cap, 2).wait()
+    join(second, cap)
+
+
+def exchange(cap, shared, collective, packed, heads, width):
+    page = packed.shape[1:]
+    count = 4 * cap + 1
+    dma = pltpu.SemaphoreType.DMA
+    return pl.pallas_call(
+        functools.partial(exchange_kernel, cap, shared),
+        out_shape=(
+            jax.ShapeDtypeStruct((count,) + page, packed.dtype),
+            jax.ShapeDtypeStruct((count, 2 * heads, width), jnp.float32),
+        ),
+        in_specs=[ANY],
+        out_specs=(ANY, VMEM),
+        scratch_shapes=[
+            pltpu.VMEM((count,) + page, packed.dtype),
+            pltpu.VMEM((4 * cap, 2 * heads, width), jnp.float32),
+            pltpu.VMEM((4 * cap, 2 * heads, width), jnp.float32),
+            dma((3 * cap,)),
+            dma((3 * cap,)),
+            dma((max(2 * shared, 1),)),
+            dma((cap,)),
+            dma((count,)),
+            dma((3,)),
+            dma((3,)),
+        ],
+        compiler_params=pltpu.CompilerParams(collective_id=collective, has_side_effects=True),
+    )(packed)
+
+
+def line_of_four(kv_cache, keep_list, page_slot):
+    layers, page_count = keep_list.shape
+    blk_dev = kv_cache.shape[1]
+    page = kv_cache.shape[2:]
+    heads, width = page[0], page[-1] // 2
+    page_dev = page_count // 4
+    cap = layers * ((page_dev - 2) // 4 + 2)
+    dma = pltpu.SemaphoreType.DMA
+    me = lax.axis_index("seq")
+
+    position = jnp.arange(page_count, dtype=jnp.int32)
+    counts = jnp.array(
+        [page_count - layer * page_count // (2 * layers) for layer in range(layers)], jnp.int32
+    )
+    listed = (position[None, :] < counts[:, None]).reshape(-1)
+    layer = jnp.repeat(jnp.arange(layers, dtype=jnp.int32), page_count)
+    keep = jnp.where(listed, keep_list.reshape(-1), 0)
+    slot = jnp.where(listed, page_slot.reshape(-1), 0)
+    source, owner = keep // blk_dev, slot // page_dev
+    pair = jnp.where(listed, source * 4 + owner, -1)
+    place = jnp.arange(layers * page_count, dtype=jnp.int32)
+    rank = jnp.sum(
+        (pair[:, None] == pair[None, :]) & (place[None, :] < place[:, None]), axis=1
+    ).astype(jnp.int32)
+    crossing = listed & (source // 2 != owner // 2)
+    pools = jnp.sum(
+        crossing[None, :] & (source[None, :] == jnp.arange(4, dtype=jnp.int32)[:, None]), axis=1
+    )
+    largest = jnp.max(pools).astype(jnp.int32).reshape(1)
+    if lax.axis_size("groups") > 1:
+        size = lax.axis_size("groups")
+        told = largest
+        for step in range(1, size):
+            passed = lax.ppermute(told, "groups", [(i, (i + step) % size) for i in range(size)])
+            largest = jnp.maximum(largest, passed)
+    sizes = [s for s in SHARED if s <= cap]
+    fits = sum((largest[0] <= 2 * cap - s).astype(jnp.int32) for s in sizes)
+    shared = jnp.array([0] + sizes, jnp.int32)[fits]
+    alone = cap - shared
+
+    to_far = crossing & ((owner == 0) | (owner == 3))
+    spill = rank - alone
+    lone = rank < alone
+    in_region = jnp.where(
+        crossing,
+        jnp.where(lone, shared + rank, jnp.where(to_far, shared - 1 - spill, spill)),
+        rank,
+    )
+    sent = jnp.where(
+        crossing,
+        in_region + jnp.where(to_far & lone, alone, 0),
+        in_region + jnp.where(source == owner, 3 * cap, 2 * cap),
+    )
+    got = in_region + jnp.where(
+        crossing, (source % 2) * cap, jnp.where(source == owner, 3 * cap, 2 * cap)
+    )
+    spots = jnp.arange(4 * cap, dtype=jnp.int32)
+    from_me = listed & (source == me)
+    pack_table = jnp.sum(
+        jnp.where(
+            from_me[None, :] & (sent[None, :] == spots[:, None]),
+            (layer * blk_dev + keep % blk_dev)[None, :],
+            0,
+        ),
+        axis=1,
+    ).astype(jnp.int32)
+    pages = jnp.arange(layers * page_dev, dtype=jnp.int32)
+    to_me = listed & (owner == me)
+    place_table = 4 * cap + jnp.sum(
+        jnp.where(
+            to_me[None, :] & ((layer * page_dev + slot % page_dev)[None, :] == pages[:, None]),
+            (got - 4 * cap)[None, :],
+            0,
+        ),
+        axis=1,
+    ).astype(jnp.int32)
+
+    packed = pl.pallas_call(
+        pack_kernel,
+        out_shape=jax.ShapeDtypeStruct((4 * cap,) + page, kv_cache.dtype),
+        in_specs=[SMEM, ANY],
+        out_specs=ANY,
+        scratch_shapes=[
+            pltpu.VMEM((4 * cap,) + page, kv_cache.dtype),
+            dma((4 * cap,)),
+            dma((4 * cap,)),
+        ],
+    )(pack_table, kv_cache.reshape((layers * blk_dev,) + page))
+
+    slots, bounds = lax.switch(
+        fits,
+        [
+            functools.partial(exchange, cap, s, k, heads=heads, width=width)
+            for k, s in enumerate([0] + sizes)
+        ],
+        packed,
+    )
+
+    paged, page_bounds = pl.pallas_call(
+        place_kernel,
+        out_shape=(
+            jax.ShapeDtypeStruct((layers * page_dev,) + page, kv_cache.dtype),
+            jax.ShapeDtypeStruct((layers * page_dev, 2 * heads, width), jnp.float32),
+        ),
+        in_specs=[SMEM, ANY, VMEM],
+        out_specs=(ANY, VMEM),
+        scratch_shapes=[
+            pltpu.VMEM((layers * page_dev,) + page, kv_cache.dtype),
+            dma((layers * page_dev,)),
+            dma((layers * page_dev,)),
+        ],
+    )(place_table, slots, bounds)
+    page_bounds = page_bounds.reshape(layers, page_dev, 2, heads, width)
+    return (
+        paged.reshape((layers, page_dev) + page),
+        page_bounds.transpose(0, 1, 3, 2, 4).astype(kv_cache.dtype),
+    )
+
+
+def on_device(kv_cache, keep_list, page_slot):
+    body = line_of_four if lax.axis_size("seq") == 4 else any_line
+    return body(kv_cache, keep_list, page_slot)
+
+
 def solution(mesh):
     in_specs = (
         P(None, ("groups", "seq"), "head", "rep", None),

time: 170 us -> 125 us (0.74)
  waiting for transfers between devices: 116 us -> 1.27 us
  Pallas kernels: 0 us -> 108 us
  matrix products: 17.8 us -> 0 us
  local copies, waits for them, and re-layouts: 21.2 us -> 3.69 us
  blocking collectives: 3.71 us -> 0 us
  starting transfers between devices: 6.48 us -> 3 us
  between operations: 0.69 us -> 3.34 us
    all_to_all x1 -> x0, waiting for transfers between devices: 116 us -> none  [on_device(): lax.all_to_all(packed, 'seq', split_axis=1, concat_axis=1, tiled=True)]
    pallas_call x0 -> x3, Pallas kernels: none -> 108 us  [the longest x1 96.3 us: exchange(): pl.pallas_call(functools.partial(exchange_kernel, cap, shared), out_shape...]
    dot_general x2 -> x0, matrix products: 17.8 us -> none  [the longest x1 9.26 us: place_pages(): jnp.einsum('lpn,lnr->lpr', one_hot, shard_part, preferred_element_type=jn...]
    reshape x1 -> x2, local copies, waits for them, and re-layouts: 10.6 us -> 1.52 us  [the longest x1 0.76 us: line_of_four(): keep = jnp.where(listed, keep_list.reshape(-1), 0)]
    convert_element_type x1, local copies, waits for them, and re-layouts: 8.97 us -> 0.68 us  [line_of_four(): page_bounds.transpose(0, 1, 3, 2, 4).astype(kv_cache.dtype)]
    all_to_all x1 -> x0, starting transfers between devices: 6.48 us -> none  [on_device(): lax.all_to_all(packed, 'seq', split_axis=1, concat_axis=1, tiled=True)]
    all_gather x2 -> x0, blocking collectives: 3.71 us -> none  [combined_all(): gathered = jax.tree.map(lambda a: lax.all_gather(a, axis), part)]
    ppermute x0 -> x1, starting transfers between devices: none -> 3 us  [line_of_four(): lax.ppermute(told, 'groups', [(i, (i + step) % size) for i in range(size)])]
where the time goes in v1:
time: 125 us; the launch traced here: 124 us
  Pallas kernels  108 us (86%)
  other arithmetic  4.63 us (4%)
  local copies, waits for them, and re-layouts  3.69 us (3%)
  between operations  3.34 us (3%)
  starting transfers between devices  3 us (2%)
  waiting for transfers between devices  1.27 us (1%)
    pallas_call x1, Pallas kernels, exchange(): pl.pallas_call(functools.partial(exchange_kernel, cap, shared), out_shape...  96.3 us
    pallas_call x1, Pallas kernels, line_of_four(): pl.pallas_call(pack_kernel, out_shape=jax.ShapeDtypeStruct((4 * cap,) + p...  6.34 us
    pallas_call x1, Pallas kernels, line_of_four(): pl.pallas_call(place_kernel, out_shape=(jax.ShapeDtypeStruct((layers * pa...  5.77 us
    ppermute x1, starting transfers between devices, line_of_four(): lax.ppermute(told, 'groups', [(i, (i + step) % size) for i in range(size)])  3 us
  transfers between devices with their start and end apart: 1, of which 1 were waited for; matrix products, arithmetic and copies ran while one was open for 0% of the time, Pallas kernels for 0%

profile of v1, /device:TPU:0, one launch (start us, length us, event | category | flops | bytes accessed | tf_op | source)
XLA Modules:
  0.0 124.4 jit_solution(11592291548925788390)
XLA Ops:
  0.6 0.8 reshape.339
  1.4 0.8 reshape.338
  2.2 0.7 iota_compare_fusion.4
  2.9 0.1 lt.95
  3.0 0.1 convert_reduce_fusion.1
  3.1 0.6 reduce_max.9
  3.8 3.0 %collective-permute-start = (s32[1]{0:T(128)}, s32[1]{0:T(128)}, u32[]{:S(2)}, u32[]{:S(2)}) collective-permute-start(s32[1]{0:T(128)} %bitcast), channel_id=1, source_target_pairs={{0,16},{16,0},{1,17},{17,1},{2,18},{18,2},{3,19},{19,3},{4,20},{20... | collective-permute-start | bytes 20 | tf_op jit(solution)/shard_map/ppermute | solution.py:405
  6.8 0.1 mul.45
  6.8 0.1 mul.50
  6.9 0.2 convert_reduce_fusion
  7.1 1.3 %collective-permute-done = s32[1]{0:T(128)} collective-permute-done((s32[1]{0:T(128)}, s32[1]{0:T(128)}, u32[]{:S(2)}, u32[]{:S(2)}) %collective-permute-start) | collective-permute-done | bytes 36 | tf_op jit(solution)/shard_map/ppermute | solution.py:405
  9.7 1.2 %dynamic_slice.3 = s32[1]{0:T(128)} dynamic-slice(s32[5]{0:T(128)} %constant.120.clone, s32[]{:T(128)S(6)} %select_n.255), dynamic_slice_sizes={1} | dynamic-slice | bytes 12 | tf_op jit(solution)/shard_map/dynamic_slice | solution.py:409
  12.3 0.7 fusion.10
  13.0 0.1 select_reduce_fusion.1
  13.1 0.5 broadcast_add_fusion.table
  13.6 0.7 select_reduce_fusion.table
  14.3 6.3 %shard_map.68 = bf16[40,4,64,256]{3,2,1,0:T(8,128)(2,1)} custom-call(s32[40]{0:T(128)} %select_reduce_fusion.table, bf16[64,4,64,256]{3,2,1,0:T(8,128)(2,1)} %bitcast.9), custom_call_target="tpu_custom_call" | custom-call | tf_op jit(solution)/shard_map/pallas_call | solution.py:449
  20.7 96.3 %conditional.1 = ((bf16[41,4,64,256]{3,2,1,0:T(8,128)(2,1)}, f32[41,8,128]{2,1,0:T(8,128)S(1)})) conditional(s32[]{:T(128)} %clamp.3, bf16[40,4,64,256]{3,2,1,0:T(8,128)(2,1)} %shard_map.68, bf16[40,4,64,256]{3,2,1,0:T(8,128)(2,1)} %shard_map.68, bf16[40,4,64,256]{3,2,1,0:T(8,128)(2,1)} %shard_map.68, ...), branch_computations={%region_5.6_spmd, %region_6.7_spmd, %region_7.8_spmd, %region_8.9_... | conditional | bytes 8 | solution.py:461
  20.7 96.3 %branch_3_fun.1 = (bf16[41,4,64,256]{3,2,1,0:T(8,128)(2,1)}, f32[41,8,128]{2,1,0:T(8,128)S(1)}) custom-call(bf16[40,4,64,256]{3,2,1,0:T(8,128)(2,1)} %packed.3), custom_call_target="tpu_custom_call" | custom-call | tf_op jit(solution)/shard_map/cond/branch_3_fun/pallas_call | solution.py:348
  117.0 5.8 %shard_map.69 = (bf16[32,4,64,256]{3,2,1,0:T(8,128)(2,1)}, f32[32,8,128]{2,1,0:T(8,128)}) custom-call(s32[32]{0:T(128)} %broadcast_add_fusion.table, bf16[41,4,64,256]{3,2,1,0:T(8,128)(2,1)} %get-tuple-element.11.slots, f32[41,8,128]{2,1,0:T(8,128)S(1)} %get-tuple-element.12.bounds), custom_call_target="tpu_custom_call" | custom-call | tf_op jit(solution)/shard_map/pallas_call | solution.py:470
  122.8 0.9 convert_element_type.40
  123.7 0.7 copy.10
  (6 shorter events, 0.1 us)
Async XLA Ops:
  3.8 4.6 %collective-permute-start = (s32[1]{0:T(128)}, s32[1]{0:T(128)}, u32[]{:S(2)}, u32[]{:S(2)}) collective-permute-start(s32[1]{0:T(128)} %bitcast), channel_id=1, source_target_pairs={{0,16},{16,0},{1,17},{17,1},{2,18},{18,2},{3,19},{19,3},{4,20},{20... | collective-permute-start | bytes 20 | tf_op jit(solution)/shard_map/ppermute | solution.py:405
